TPU v7x, 128 devices: a whole 4x4x4 slice. The times are simulated.
128 devices in a mesh: dp: 1, cp: 128 (over z, y, x, core).
Axes of the slice: x: 4, y: 4, z: 4, core: 2. Of those that a mesh axis runs over, the one named last changes fastest.
Arguments:
- x_in: bfloat16 [2048, 5120], P(('dp', 'cp'))
- dy_in: bfloat16 [2048, 5120], P(('dp', 'cp'))
- w_q: bfloat16 [5120, 40, 128], replicated
- w_k: bfloat16 [5120, 40, 128], replicated
- w_v: bfloat16 [5120, 40, 128], replicated
- w_o: bfloat16 [40, 128, 5120], replicated
Outputs:
- output 1: bfloat16 [2048, 5120], P(('dp', 'cp'))
- output 2: bfloat16 [2048, 5120], P(('dp', 'cp'))
All inputs are finite; a program needn't handle non-finite values.
Results may differ from a plain program's by a relative error of at most 0.0107894.
Values are sent between devices in bfloat16 or wider.
A program may use at most 1 GiB of HBM per device.

v0:
```python
import jax
import jax.numpy as jnp
from jax import lax
from jax.sharding import PartitionSpec as P


def local_positions(dev_index, group_devs, tok_dev):
    half_len = tok_dev // 2
    offsets = jnp.arange(half_len, dtype=jnp.int32)
    first_pos = dev_index * half_len + offsets
    second_pos = (2 * group_devs - 1 - dev_index) * half_len + offsets
    return jnp.concatenate([first_pos, second_pos], axis=-1)


def all_positions(group_devs, tok_dev):
    dev_ids = jnp.arange(group_devs, dtype=jnp.int32)[:, None]
    return local_positions(dev_ids, group_devs, tok_dev).reshape(group_devs * tok_dev)


def solution(mesh):
    group_devs = mesh.shape["cp"]

    def attend_layer(x_loc, dy_loc, w_q, w_k, w_v, w_o):
        tok_dev = x_loc.shape[0]
        head_dim = w_q.shape[2]
        score_scale = head_dim ** -0.5
        dev_index = lax.axis_index("cp")
        q_pos = local_positions(dev_index, group_devs, tok_dev)
        key_pos = all_positions(group_devs, tok_dev)
        causal = (q_pos[:, None] >= key_pos[None, :])[None]

        def project(weight):
            return jnp.einsum("td,dhe->hte", x_loc, weight,
                              preferred_element_type=jnp.float32).astype(jnp.bfloat16)

        q_loc = project(w_q)
        k_loc = project(w_k)
        v_loc = project(w_v)
        k_all = lax.all_gather(k_loc, "cp", axis=1, tiled=True)
        v_all = lax.all_gather(v_loc, "cp", axis=1, tiled=True)
        scores = jnp.einsum("hqe,hke->hqk", q_loc, k_all, preferred_element_type=jnp.float32) * score_scale
        scores = jnp.where(causal, scores, -jnp.inf)
        log_norm = jax.nn.logsumexp(scores, axis=-1, keepdims=True)
        attn_probs = jnp.exp(scores - log_norm).astype(jnp.bfloat16)
        attn_out = jnp.einsum("hqk,hke->hqe", attn_probs, v_all,
                              preferred_element_type=jnp.float32).astype(jnp.bfloat16)
        y_loc = jnp.einsum("hte,hed->td", attn_out, w_o, preferred_element_type=jnp.float32).astype(jnp.bfloat16)
        d_out = jnp.einsum("td,hed->hte", dy_loc, w_o, preferred_element_type=jnp.float32).astype(jnp.bfloat16)
        row_delta = jnp.einsum("hqe,hqe->hq", d_out, attn_out, preferred_element_type=jnp.float32)[..., None]
        d_probs = jnp.einsum("hqe,hke->hqk", d_out, v_all, preferred_element_type=jnp.float32)
        d_scores = (attn_probs * (d_probs - row_delta)).astype(jnp.bfloat16)
        d_query = (jnp.einsum("hqk,hke->hqe", d_scores, k_all, preferred_element_type=jnp.float32)
                   * score_scale).astype(jnp.bfloat16)
        dk_part = jnp.einsum("hqk,hqe->hke", d_scores, q_loc, preferred_element_type=jnp.float32) * score_scale
        dv_part = jnp.einsum("hqk,hqe->hke", attn_probs, d_out, preferred_element_type=jnp.float32)
        dk_loc = lax.psum_scatter(dk_part, "cp", scatter_dimension=1, tiled=True).astype(jnp.bfloat16)
        dv_loc = lax.psum_scatter(dv_part, "cp", scatter_dimension=1, tiled=True).astype(jnp.bfloat16)
        dx_acc = (jnp.einsum("hte,dhe->td", d_query, w_q, preferred_element_type=jnp.float32)
                  + jnp.einsum("hte,dhe->td", dk_loc, w_k, preferred_element_type=jnp.float32)
                  + jnp.einsum("hte,dhe->td", dv_loc, w_v, preferred_element_type=jnp.float32))
        return y_loc, dx_acc.astype(jnp.bfloat16)

    row_spec = P(("dp", "cp"), None)
    full_spec = P(None, None, None)
    return jax.shard_map(
        attend_layer, mesh=mesh,
        in_specs=(row_spec, row_spec, full_spec, full_spec, full_spec, full_spec),
        out_specs=(row_spec, row_spec), check_vma=False)
```

profile of v0, /device:TPU:0, one launch (start us, length us, event | category | flops | bytes accessed | tf_op | source)
XLA Modules:
  0.0 1739.3 jit_solution(18047025407847116715)
XLA Ops:
  7.2 0.0 copy-start
  7.2 0.0 all-gather.3.cloned.1.call-start
  7.2 0.9 copy-done
  8.1 21.1 %fusion.45 = bf16[40,16,128]{2,1,0:T(8,128)(2,1)} fusion(bf16[5120,40,128]{2,1,0:T(8,128)(2,1)} %param.9, bf16[16,5120]{1,0:T(8,128)(2,1)S(1)} %copy-done), kind=kOutput, calls=%fused_computation.34 | convolution fusion | flops 838942720 | bytes 52756480 | tf_op jit(solution)/shard_map/td,dhe->hte/dot_general | solution.py:33
  29.2 0.0 all-gather.3.cloned.1.call-update
  29.2 0.0 all-gather.5.cloned.1.call-start
  29.2 21.1 %fusion.42 = bf16[40,16,128]{2,1,0:T(8,128)(2,1)} fusion(bf16[5120,40,128]{2,1,0:T(8,128)(2,1)} %param.10, bf16[16,5120]{1,0:T(8,128)(2,1)S(1)} %copy-done), kind=kOutput, calls=%fused_computation.33 | convolution fusion | flops 838942720 | bytes 52756480 | tf_op jit(solution)/shard_map/td,dhe->hte/dot_general | solution.py:33
  50.3 0.0 all-gather.5.cloned.1.call-update
  50.4 0.2 reduce-scatter.3.cloned.1.call-start
  50.6 0.1 copy.20
  50.7 0.1 ge.20
  50.8 0.1 pad_add_fusion.1
  50.9 0.1 broadcast_compare_fusion
  51.0 0.0 copy-start.5
  51.0 20.5 %fusion.33 = bf16[40,128,16]{1,2,0:T(8,128)(2,1)S(1)} fusion(bf16[5120,40,128]{2,1,0:T(8,128)(2,1)} %param.8, bf16[16,5120]{1,0:T(8,128)(2,1)S(1)} %copy-done), kind=kOutput, calls=%fused_computation.28 | convolution fusion | flops 838942720 | bytes 52756480 | tf_op jit(solution)/shard_map/td,dhe->hte/dot_general | solution.py:33
  71.5 0.0 copy-done.5
  71.5 21.0 %convolution_convert_fusion = bf16[40,128,16]{1,2,0:T(8,128)(2,1)S(1)} fusion(bf16[40,128,5120]{2,1,0:T(8,128)(2,1)} %param.11, bf16[16,5120]{1,0:T(8,128)(2,1)S(1)} %copy-done.5), kind=kOutput, calls=%fused_computation.31 | convolution fusion | flops 838942720 | bytes 52756480 | tf_op jit(solution)/shard_map/td,hed->hte/dot_general | solution.py:48
  92.5 48.7 %all-gather.3.cloned.1.call-done = bf16[40,2048,128]{2,1,0:T(8,128)(2,1)} async-done(((bf16[40,16,128]{2,1,0:T(8,128)(2,1)}), bf16[40,2048,128]{2,1,0:T(8,128)(2,1)}) %all-gather.3.cloned.1.call-update) | async-done | bytes 20971536 | tf_op jit(solution)/shard_map/all_gather | solution.py:39
  141.2 9.9 fusion.31
  151.1 0.0 copy-start.2
  151.1 1.2 exponential_reduce_fusion
  152.3 1.1 copy-done.2
  153.4 3.5 exponential_convert_fusion
  156.9 98.0 %all-gather.5.cloned.1.call-done = bf16[40,2048,128]{2,1,0:T(8,128)(2,1)} async-done(((bf16[40,16,128]{2,1,0:T(8,128)(2,1)}), bf16[40,2048,128]{2,1,0:T(8,128)(2,1)}) %all-gather.5.cloned.1.call-update) | async-done | bytes 20971536 | tf_op jit(solution)/shard_map/all_gather | solution.py:40
  254.9 8.6 fusion.48
  263.5 9.8 multiply_convert_fusion
  273.4 0.0 copy-start.3
  273.4 1.5 copy-done.3
  274.8 14.9 broadcast_multiply_fusion
  289.8 0.0 reduce-scatter.3.cloned.1.call-update
  289.8 0.0 reduce-scatter.5.cloned.1.call-start
  289.8 15.3 fusion.57
  305.1 0.0 copy-start.4
  305.1 0.0 reduce-scatter.5.cloned.1.call-update
  305.1 1.7 copy-done.4
  306.8 8.5 fusion.32.clone.4
  315.3 20.4 %fusion.12 = f32[16,5120]{1,0:T(8,128)S(1)} fusion(bf16[5120,40,128]{2,1,0:T(8,128)(2,1)} %param.8, bf16[40,16,128]{2,1,0:T(8,128)(2,1)S(1)} %fusion.32.clone.4), kind=kOutput, calls=%fused_computation.14 | convolution fusion | flops 838860800 | bytes 52920320 | tf_op jit(solution)/shard_map/hte,dhe->td/dot_general | solution.py:58
  335.8 18.7 %fusion.27 = bf16[16,5120]{1,0:T(8,128)(2,1)} fusion(bf16[40,16,128]{2,1,0:T(8,128)(2,1)S(1)} %get-tuple-element.5, bf16[40,128,5120]{2,1,0:T(8,128)(2,1)} %param.11), kind=kOutput, calls=%fused_computation.19 | convolution fusion | flops 838942720 | bytes 52756480 | tf_op jit(solution)/shard_map/hte,hed->td/dot_general | solution.py:47
  354.4 648.8 %reduce-scatter.3.cloned.1.call-done = f32[40,16,128]{2,1,0:T(8,128)} async-done(((f32[40,2048,128]{2,1,0:T(8,128)}), f32[40,16,128]{2,1,0:T(8,128)}) %reduce-scatter.3.cloned.1.call-update) | async-done | bytes 327696 | tf_op jit(solution)/shard_map/reduce_scatter | solution.py:56
  1003.2 0.0 copy-start.1
  1003.2 20.8 %fusion.24 = f32[16,5120]{1,0:T(8,128)S(1)} fusion(f32[16,5120]{1,0:T(8,128)S(1)} %fusion.12, bf16[5120,40,128]{2,1,0:T(8,128)(2,1)} %param.9, f32[40,16,128]{2,1,0:T(8,128)} %reduce-scatter.3.cloned.1.call-done), kind=kOutput, calls=%fused_computation.18 | convolution fusion | flops 839024640 | bytes 53411840 | tf_op jit(solution)/shard_map/hte,dhe->td/dot_general | solution.py:59
  1024.0 687.1 %reduce-scatter.5.cloned.1.call-done = f32[40,16,128]{2,1,0:T(8,128)} async-done(((f32[40,2048,128]{2,1,0:T(8,128)}), f32[40,16,128]{2,1,0:T(8,128)}) %reduce-scatter.5.cloned.1.call-update) | async-done | bytes 327696 | tf_op jit(solution)/shard_map/reduce_scatter | solution.py:57
  1711.1 21.2 %fusion.28 = bf16[16,5120]{1,0:T(8,128)(2,1)} fusion(f32[16,5120]{1,0:T(8,128)S(1)} %fusion.24, bf16[5120,40,128]{2,1,0:T(8,128)(2,1)} %param.10, f32[40,16,128]{2,1,0:T(8,128)} %reduce-scatter.5.cloned.1.call-done), kind=kOutput, calls=%fused_computation.20 | convolution fusion | flops 839106560 | bytes 53248000 | tf_op jit(solution)/shard_map/hte,dhe->td/dot_general | solution.py:60
  1732.3 0.0 copy-done.1
  (7 shorter events, 0.0 us)
Async XLA Ops:
  7.2 0.9 copy-start
  7.2 134.0 %all-gather.3.cloned.1.call-start = ((), (), s32[]{:S(2)}) async-start(), calls=%async_computation.2 | async-start | bytes 21135360 | tf_op jit(solution)/shard_map/all_gather | solution.py:39
  29.2 225.7 %all-gather.5.cloned.1.call-start = ((), (), s32[]{:S(2)}) async-start(), calls=%async_computation.3 | async-start | bytes 21135360 | tf_op jit(solution)/shard_map/all_gather | solution.py:40
  50.4 952.9 %reduce-scatter.3.cloned.1.call-start = ((), (), s32[]{:S(2)}) async-start(), calls=%async_computation.4 | async-start | bytes 42270720 | tf_op jit(solution)/shard_map/reduce_scatter | solution.py:56
  51.0 20.5 %copy-start.5 = (bf16[16,5120]{1,0:T(8,128)(2,1)S(1)}, bf16[16,5120]{1,0:T(8,128)(2,1)}, u32[]{:S(2)}) copy-start(bf16[16,5120]{1,0:T(8,128)(2,1)} %param.7) | copy-start | bytes 491524
  151.1 2.3 copy-start.2
  273.4 1.5 copy-start.3
  289.8 1421.3 %reduce-scatter.5.cloned.1.call-start = ((), (), s32[]{:S(2)}) async-start(), calls=%async_computation.5 | async-start | bytes 42270720 | tf_op jit(solution)/shard_map/reduce_scatter | solution.py:57
  305.1 1.7 copy-start.4
  1003.2 729.0 %copy-start.1 = (bf16[16,5120]{1,0:T(8,128)(2,1)S(1)}, bf16[16,5120]{1,0:T(8,128)(2,1)}, u32[]{:S(2)}) copy-start(bf16[16,5120]{1,0:T(8,128)(2,1)} %param.6) | copy-start | bytes 491524
Sparse Core Ops, SparseCore 0:
  29.3 111.8 all-gather.2
  144.6 110.2 all-gather.4
  289.9 713.2 reduce-scatter.2
  1005.5 705.5 reduce-scatter.4
where the time goes:
time: 1750 us; the launch traced here: 1740 us
  waiting for transfers between devices  1480 us (85%)
  matrix products  232 us (13%)
    reduce_scatter x1, waiting for transfers between devices, attend_layer(): lax.psum_scatter(dv_part, 'cp', scatter_dimension=1, tiled=True)  687 us
    reduce_scatter x1, waiting for transfers between devices, attend_layer(): lax.psum_scatter(dk_part, 'cp', scatter_dimension=1, tiled=True)  649 us
    all_gather x1, waiting for transfers between devices, attend_layer(): v_all = lax.all_gather(v_loc, 'cp', axis=1, tiled=True)  98 us
    dot_general x3, matrix products, project(): jnp.einsum('td,dhe->hte', x_loc, weight, preferred_element_type=jnp.float32)  62.6 us
    all_gather x1, waiting for transfers between devices, attend_layer(): k_all = lax.all_gather(k_loc, 'cp', axis=1, tiled=True)  48.7 us
  transfers between devices with their start and end apart: 4, of which 4 were waited for; matrix products, arithmetic and copies ran while one was open for 9% of the time, Pallas kernels for 0%

commit v1 on v0

v1 whole, which is shorter than its diff:
```python
import functools

import jax
import jax.numpy as jnp
from jax import lax
from jax.experimental import pallas as pl
from jax.experimental.pallas import tpu as pltpu
from jax.sharding import PartitionSpec as P

LOG2E = 1.4426950408889634
QB, KB = 512, 256
F32 = jnp.float32
BF16 = jnp.bfloat16


def head_home(h, heads, devs):
    return (h * (devs // 2) // heads) * 2 + 1


def home_head(me, heads, devs):
    chips = devs // 2
    chip = me // 2
    h = (chip * heads + chips - 1) // chips
    has = (me % 2 == 1) & (h < heads) & ((h * chips) // heads == chip)
    return h, has


def gather_kernel(heads, devs, src, dst, send_sem, recv_sem):
    me = lax.axis_index("cp")
    _, has = home_head(me, heads, devs)

    def send(n, carry):
        h = lax.rem(n + me, heads)
        home = head_home(h, heads, devs)
        for side in range(2):
            piece = me if side == 0 else 2 * devs - 1 - me

            @pl.when(home != me)
            def _():
                pltpu.make_async_remote_copy(
                    src_ref=src.at[h, :, side], dst_ref=dst.at[:, piece],
                    send_sem=send_sem, recv_sem=recv_sem,
                    device_id={"cp": home}, device_id_type=pl.DeviceIdType.MESH).start()

            @pl.when(home == me)
            def _():
                pltpu.make_async_copy(src.at[h, :, side], dst.at[:, piece], recv_sem).start()

        return carry

    lax.fori_loop(0, heads, send, 0)

    @pl.when(has)
    def _():
        sent = src.at[pl.ds(0, heads - 1)]
        pltpu.make_async_copy(sent, sent, send_sem).wait()
        pltpu.make_async_copy(dst, dst, recv_sem).wait()

    @pl.when(jnp.logical_not(has))
    def _():
        pltpu.make_async_copy(src, src, send_sem).wait()


def scatter_kernel(heads, devs, src, dst, send_sem, recv_sem):
    me = lax.axis_index("cp")
    mine, has = home_head(me, heads, devs)

    @pl.when(has)
    def _():
        def send(n, carry):
            to = lax.rem(n + 1 + me, devs)
            for side in range(2):
                piece = to if side == 0 else 2 * devs - 1 - to
                pltpu.make_async_remote_copy(
                    src_ref=src.at[:, piece], dst_ref=dst.at[mine, :, side],
                    send_sem=send_sem, recv_sem=recv_sem,
                    device_id={"cp": to}, device_id_type=pl.DeviceIdType.MESH).start()
            return carry

        for side in range(2):
            piece = me if side == 0 else 2 * devs - 1 - me
            pltpu.make_async_copy(src.at[:, piece], dst.at[mine, :, side], recv_sem).start()
        lax.fori_loop(0, devs - 1, send, 0)

    pltpu.make_async_copy(dst, dst, recv_sem).wait()

    @pl.when(has)
    def _():
        sent = src.at[:, pl.ds(0, 2 * devs - 2)]
        pltpu.make_async_copy(sent, sent, send_sem).wait()


def dot(a, b, dims):
    return lax.dot_general(a, b, (dims, ((), ())), preferred_element_type=F32)


NN = ((1,), (0,))
NT = ((1,), (1,))


def attend_kernel(heads, devs, qb, kb, x_ref, out_ref, kt, vt, dot_t, s_scr, p_scr, dk_acc, dv_acc, oq_scr):
    me = lax.axis_index("cp")
    _, has = home_head(me, heads, devs)
    seq, e = x_ref.shape[1], x_ref.shape[2]
    c = e ** -0.5
    k2 = c * LOG2E
    nqb = seq // qb
    per = qb // kb

    @pl.when(has)
    def _():
        def prep(i, carry):
            rows = pl.ds(pl.multiple_of(i * kb, kb), kb)
            kt[:, rows] = x_ref[1, rows, :].T
            vt[:, rows] = x_ref[2, rows, :].T
            dot_t[:, rows] = x_ref[3, rows, :].T
            dk_acc[rows, :] = jnp.zeros((kb, e), F32)
            dv_acc[rows, :] = jnp.zeros((kb, e), F32)
            return carry

        lax.fori_loop(0, seq // kb, prep, 0)

        def q_block(i, carry):
            qrows = pl.ds(pl.multiple_of(i * qb, qb), qb)
            q = x_ref[0, qrows, :]
            do = x_ref[3, qrows, :]
            full = i * per

            def krows(j):
                return pl.ds(pl.multiple_of(j * kb, kb), kb)

            def scores(j, m, masked):
                s = dot(x_ref[1, krows(j), :], q, NT)
                if masked:
                    kpos = j * kb + lax.broadcasted_iota(jnp.int32, (kb, qb), 0)
                    qpos = i * qb + lax.broadcasted_iota(jnp.int32, (kb, qb), 1)
                    s = jnp.where(qpos >= kpos, s, -jnp.inf)
                s_scr[krows(j), :] = s
                return jnp.maximum(m, jnp.max(s.reshape(kb // 8, 8, qb), axis=0))

            m8 = jnp.full((8, qb), -jnp.inf, F32)
            m8 = lax.fori_loop(0, full, lambda j, m: scores(j, m, False), m8)
            for d in range(per):
                m8 = scores(full + d, m8, True)
            m = jnp.max(m8, axis=0, keepdims=True) * k2

            def exps(j, l):
                p = jnp.exp2(s_scr[krows(j), :] * k2 - m)
                s_scr[krows(j), :] = p
                return l + jnp.sum(p.reshape(kb // 8, 8, qb), axis=0)

            l8 = lax.fori_loop(0, full + per, exps, jnp.zeros((8, qb), F32))
            inv = 1.0 / jnp.sum(l8, axis=0, keepdims=True)

            oq_scr[...] = jnp.zeros_like(oq_scr)

            def probs(j, carry):
                p = (s_scr[krows(j), :] * inv).astype(BF16)
                p_scr[krows(j), :] = p
                oq_scr[...] += dot(vt[:, krows(j)], p, NN)
                return carry

            lax.fori_loop(0, full + per, probs, 0)
            o_t = oq_scr[...].astype(BF16)
            delta = jnp.sum(o_t.astype(F32) * dot_t[:, qrows].astype(F32), axis=0, keepdims=True)
            out_ref[0, qrows, :] = o_t.T
            oq_scr[...] = jnp.zeros_like(oq_scr)

            def back(j, carry):
                p = p_scr[krows(j), :]
                dp = dot(x_ref[2, krows(j), :], do, NT)
                ds = (p.astype(F32) * (dp - delta)).astype(BF16)
                dv_acc[krows(j), :] += dot(p, do, NN)
                dk_acc[krows(j), :] += dot(ds, q, NN)
                oq_scr[...] += dot(kt[:, krows(j)], ds, NN)
                return carry

            lax.fori_loop(0, full + per, back, 0)
            out_ref[1, qrows, :] = (oq_scr[...] * c).astype(BF16).T
            return carry

        lax.fori_loop(0, nqb, q_block, 0)

        def finish(i, carry):
            rows = pl.ds(pl.multiple_of(i * kb, kb), kb)
            out_ref[2, rows, :] = (dk_acc[rows, :] * c).astype(BF16)
            out_ref[3, rows, :] = dv_acc[rows, :].astype(BF16)
            return carry

        lax.fori_loop(0, seq // kb, finish, 0)


def solution(mesh):
    devs = mesh.shape["cp"]

    def attend_layer(x_loc, dy_loc, w_q, w_k, w_v, w_o):
        tok = x_loc.shape[0]
        half = tok // 2
        heads, e = w_q.shape[1:]
        seq = devs * tok
        qb = min(QB, seq)
        kb = min(KB, seq)

        def project(weight):
            return jnp.einsum("td,dhe->hte", x_loc, weight, preferred_element_type=F32).astype(BF16)

        d_out = jnp.einsum("td,hed->hte", dy_loc, w_o, preferred_element_type=F32).astype(BF16)
        packed = jnp.stack([project(w_q), project(w_k), project(w_v), d_out], axis=1)
        packed = packed.reshape(heads, 4, 2, half, e)
        hbm = pl.BlockSpec(memory_space=pl.ANY)
        sems = [pltpu.SemaphoreType.DMA, pltpu.SemaphoreType.DMA]
        by_head = pl.pallas_call(
            functools.partial(gather_kernel, heads, devs),
            out_shape=jax.ShapeDtypeStruct((4, 2 * devs, half, e), BF16),
            in_specs=[hbm], out_specs=hbm, scratch_shapes=sems, name="rows_to_heads",
            compiler_params=pltpu.CompilerParams(has_side_effects=True))(packed)
        vmem = pl.BlockSpec(memory_space=pltpu.VMEM)
        grads = pl.pallas_call(
            functools.partial(attend_kernel, heads, devs, qb, kb),
            out_shape=jax.ShapeDtypeStruct((4, seq, e), BF16),
            in_specs=[vmem], out_specs=vmem, name="attend",
            scratch_shapes=[
                pltpu.VMEM((e, seq), BF16), pltpu.VMEM((e, seq), BF16), pltpu.VMEM((e, seq), BF16),
                pltpu.VMEM((seq, qb), F32), pltpu.VMEM((seq, qb), BF16),
                pltpu.VMEM((seq, e), F32), pltpu.VMEM((seq, e), F32), pltpu.VMEM((e, qb), F32)],
            compiler_params=pltpu.CompilerParams(vmem_limit_bytes=48 << 20))(by_head.reshape(4, seq, e))
        back = pl.pallas_call(
            functools.partial(scatter_kernel, heads, devs),
            out_shape=jax.ShapeDtypeStruct((heads, 4, 2, half, e), BF16),
            in_specs=[hbm], out_specs=hbm, scratch_shapes=sems, name="heads_to_rows",
            compiler_params=pltpu.CompilerParams(has_side_effects=True))(grads.reshape(4, 2 * devs, half, e))
        back = back.reshape(heads, 4, tok, e)
        y_loc = jnp.einsum("hte,hed->td", back[:, 0], w_o, preferred_element_type=F32).astype(BF16)
        dx = (jnp.einsum("hte,dhe->td", back[:, 1], w_q, preferred_element_type=F32)
              + jnp.einsum("hte,dhe->td", back[:, 2], w_k, preferred_element_type=F32)
              + jnp.einsum("hte,dhe->td", back[:, 3], w_v, preferred_element_type=F32))
        return y_loc, dx.astype(BF16)

    row_spec = P(("dp", "cp"), None)
    full_spec = P(None, None, None)
    return jax.shard_map(
        attend_layer, mesh=mesh,
        in_specs=(row_spec, row_spec, full_spec, full_spec, full_spec, full_spec),
        out_specs=(row_spec, row_spec), check_vma=False)
```

time: 1750 us -> 243 us (0.14)
  waiting for transfers between devices: 1480 us -> 0 us
  Pallas kernels: 0 us -> 67.7 us
  matrix products: 232 us -> 168 us
    reduce_scatter x2 -> x0, waiting for transfers between devices: 1340 us -> none  [the longest x1 687 us: attend_layer(): lax.psum_scatter(dv_part, 'cp', scatter_dimension=1, tiled=True)]
    all_gather x2 -> x0, waiting for transfers between devices: 147 us -> none  [the longest x1 98 us: attend_layer(): v_all = lax.all_gather(v_loc, 'cp', axis=1, tiled=True)]
    pallas_call x0 -> x3, Pallas kernels: none -> 67.7 us  [the longest x1 46.9 us: attend_layer(): pl.pallas_call(functools.partial(scatter_kernel, heads, devs), out_shape=...]
    dot_general x14 -> x8, matrix products: 232 us -> 168 us  [the longest x3 61.5 us: project(): jnp.einsum('td,dhe->hte', x_loc, weight, preferred_element_type=F32)]
  transfers between devices with their start and end apart: 4 -> 0, of which waited for: 4 -> 0; matrix products, arithmetic and copies ran while one was open for 9% -> 0% of each run, Pallas kernels for 0% -> 0%
where the time goes in v1:
time: 243 us; the launch traced here: 240 us
  matrix products  168 us (69%)
  Pallas kernels  67.7 us (28%)
  local copies, waits for them, and re-layouts  2.93 us (1%)
    dot_general x3, matrix products, project(): jnp.einsum('td,dhe->hte', x_loc, weight, preferred_element_type=F32)  61.5 us
    pallas_call x1, Pallas kernels, attend_layer(): pl.pallas_call(functools.partial(scatter_kernel, heads, devs), out_shape=...  46.9 us
    dot_general x1, matrix products, attend_layer(): jnp.einsum('td,hed->hte', dy_loc, w_o, preferred_element_type=F32)  22.9 us
    dot_general x1, matrix products, attend_layer(): jnp.einsum('hte,dhe->td', back[:, 3], w_v, preferred_element_type=F32)  22.1 us
    pallas_call x1, Pallas kernels, attend_layer(): pl.pallas_call(functools.partial(gather_kernel, heads, devs), out_shape=j...  20.8 us
    dot_general x1, matrix products, attend_layer(): jnp.einsum('hte,dhe->td', back[:, 1], w_q, preferred_element_type=F32)  20.5 us
    dot_general x1, matrix products, attend_layer(): jnp.einsum('hte,hed->td', back[:, 0], w_o, preferred_element_type=F32)  20.4 us
    dot_general x1, matrix products, attend_layer(): jnp.einsum('hte,dhe->td', back[:, 2], w_k, preferred_element_type=F32)  20.4 us

profile of v1, /device:TPU:0, one launch (start us, length us, event | category | flops | bytes accessed | tf_op | source)
XLA Modules:
  0.0 240.1 jit_solution(17486488611757584532)
XLA Ops:
  0.6 0.0 copy-start
  0.6 22.9 %fusion.40 = bf16[40,1,2,8,128]{4,3,2,1,0:T(8,128)(2,1)S(1)} fusion(bf16[40,128,5120]{2,1,0:T(8,128)(2,1)} %param.11, bf16[16,5120]{1,0:T(8,128)(2,1)} %param.7), kind=kOutput, calls=%fused_computation.24 | convolution fusion | flops 838942720 | bytes 52756480 | tf_op jit(solution)/shard_map/td,hed->hte/dot_general | solution.py:207
  23.6 0.0 copy-done
  23.6 20.5 %fusion.47 = bf16[40,1,2,8,128]{4,3,2,1,0:T(8,128)(2,1)S(1)} fusion(bf16[5120,40,128]{2,1,0:T(8,128)(2,1)} %param.8, bf16[16,5120]{1,0:T(8,128)(2,1)S(1)} %copy-done), kind=kOutput, calls=%fused_computation.27 | convolution fusion | flops 838942720 | bytes 52756480 | tf_op jit(solution)/shard_map/td,dhe->hte/dot_general | solution.py:205
  44.0 20.6 %fusion.44 = bf16[40,1,2,8,128]{4,3,2,1,0:T(8,128)(2,1)S(1)} fusion(bf16[5120,40,128]{2,1,0:T(8,128)(2,1)} %param.9, bf16[16,5120]{1,0:T(8,128)(2,1)S(1)} %copy-done), kind=kOutput, calls=%fused_computation.26 | convolution fusion | flops 838942720 | bytes 52756480 | tf_op jit(solution)/shard_map/td,dhe->hte/dot_general | solution.py:205
  64.6 20.4 %fusion.41 = bf16[40,1,2,8,128]{4,3,2,1,0:T(8,128)(2,1)S(1)} fusion(bf16[5120,40,128]{2,1,0:T(8,128)(2,1)} %param.10, bf16[16,5120]{1,0:T(8,128)(2,1)S(1)} %copy-done), kind=kOutput, calls=%fused_computation.25 | convolution fusion | flops 838942720 | bytes 52756480 | tf_op jit(solution)/shard_map/td,dhe->hte/dot_general | solution.py:205
  85.1 0.9 pad_maximum_fusion.src
  86.0 20.8 %rows_to_heads.1 = bf16[4,256,8,128]{3,2,1,0:T(8,128)(2,1)} custom-call(bf16[40,4,2,8,128]{4,3,2,1,0:T(8,128)(2,1)} %pad_maximum_fusion.src), custom_call_target="tpu_custom_call" | custom-call | tf_op jit(solution)/shard_map/rows_to_heads/pallas_call | solution.py:212
  106.9 0.0 copy-start.2
  106.9 1.6 copy-done.2
  108.5 0.0 copy-start.3
  108.5 1.3 copy-done.3
  109.8 46.9 %heads_to_rows.1 = bf16[40,4,2,8,128]{4,3,2,1,0:T(8,128)(2,1)} custom-call(bf16[4,256,8,128]{3,2,1,0:T(8,128)(2,1)} %bitcast.68), custom_call_target="tpu_custom_call" | custom-call | tf_op jit(solution)/shard_map/heads_to_rows/pallas_call | solution.py:227
  156.7 0.0 copy-start.4
  156.7 20.4 %fusion.27 = bf16[16,5120]{1,0:T(8,128)(2,1)} fusion(bf16[40,128,5120]{2,1,0:T(8,128)(2,1)} %param.11, bf16[40,4,16,128]{3,2,1,0:T(8,128)(2,1)} %bitcast.69), kind=kOutput, calls=%fused_computation.18 | convolution fusion | flops 838942720 | bytes 52756480 | tf_op jit(solution)/shard_map/hte,hed->td/dot_general | solution.py:233
  177.1 0.0 copy-done.4
  177.1 0.0 copy-start.1
  177.1 20.5 %fusion.12 = f32[16,5120]{1,0:T(8,128)S(1)} fusion(bf16[5120,40,128]{2,1,0:T(8,128)(2,1)} %param.8, bf16[40,4,16,128]{3,2,1,0:T(8,128)(2,1)S(1)} %bitcast.70), kind=kOutput, calls=%fused_computation.13 | convolution fusion | flops 838860800 | bytes 52920320 | tf_op jit(solution)/shard_map/hte,dhe->td/dot_general | solution.py:234
  197.6 20.4 %fusion.24 = f32[16,5120]{1,0:T(8,128)S(1)} fusion(f32[16,5120]{1,0:T(8,128)S(1)} %fusion.12, bf16[5120,40,128]{2,1,0:T(8,128)(2,1)} %param.9, bf16[40,4,16,128]{3,2,1,0:T(8,128)(2,1)S(1)} %bitcast.71), kind=kOutput, calls=%fused_computation.17 | convolution fusion | flops 838942720 | bytes 53248000 | tf_op jit(solution)/shard_map/hte,dhe->td/dot_general | solution.py:235
  218.0 22.1 %fusion.28 = bf16[16,5120]{1,0:T(8,128)(2,1)} fusion(f32[16,5120]{1,0:T(8,128)S(1)} %fusion.24, bf16[5120,40,128]{2,1,0:T(8,128)(2,1)} %param.10, bf16[40,4,16,128]{3,2,1,0:T(8,128)(2,1)S(1)} %bitcast.72), kind=kOutput, calls=%fused_computation.19 | convolution fusion | flops 839024640 | bytes 53084160 | tf_op jit(solution)/shard_map/hte,dhe->td/dot_general | solution.py:236
  240.1 0.0 copy-done.1
  (1 shorter events, 0.0 us)
Async XLA Ops:
  0.6 22.9 %copy-start = (bf16[16,5120]{1,0:T(8,128)(2,1)S(1)}, bf16[16,5120]{1,0:T(8,128)(2,1)}, u32[]{:S(2)}) copy-start(bf16[16,5120]{1,0:T(8,128)(2,1)} %param.6) | copy-start | bytes 491524
  106.9 1.6 copy-start.2
  108.5 1.3 copy-start.3
  156.7 20.4 %copy-start.4 = (bf16[40,4,2,8,128]{4,3,2,1,0:T(8,128)(2,1)S(1)}, bf16[40,4,2,8,128]{4,3,2,1,0:T(8,128)(2,1)}, u32[]{:S(2)}) copy-start(bf16[40,4,2,8,128]{4,3,2,1,0:T(8,128)(2,1)} %heads_to_rows.1) | copy-start | bytes 1966084
  177.1 63.0 %copy-start.1 = (bf16[16,5120]{1,0:T(8,128)(2,1)S(1)}, bf16[16,5120]{1,0:T(8,128)(2,1)}, u32[]{:S(2)}) copy-start(bf16[16,5120]{1,0:T(8,128)(2,1)} %param.6) | copy-start | bytes 491524
